TPU v7x, 32 devices: a whole 2x2x4 slice. The times are simulated.
32 devices in a mesh: shard: 8 (over z, x), rep: 4 (over y, core).
Axes of the slice: x: 2, y: 2, z: 4, core: 2. Of those that a mesh axis runs over, the one named last changes fastest.
Arguments:
- lender_block: int32 [96, 8], P(('shard', 'rep')), may hold values from 0 to 255, as said below
- confidence: bfloat16 [96, 8, 256, 256], P(('shard', 'rep')), may hold values from 0 to 80, as said below
- lender_factors: bfloat16 [65536, 128], P('shard'), may hold values from -4 to 4
Outputs:
- borrower_factors: float32 [24576, 128], P(('shard', 'rep'))
- lender_rhs: float32 [65536, 128], P('shard')
Inputs may be any that keep to these rules, and one draw needn't show every extreme that they name: `lender_block`: within one device's 3 borrower blocks, at most 6 of the 3 x 8 entries name blocks of any one owner (block // 32), and on every device some owner is named exactly 6 times. `confidence`: about half the entries are zero; the others are positive.
All inputs are finite; a program needn't handle non-finite values.
Results may differ from a plain program's by a relative error of at most 0.0047.
Values may be sent and summed in bfloat16 or wider, within the bound.
A program may use at most 128 MiB of HBM per device.

v0:
```python
import jax
import jax.numpy as jnp
from jax import lax
from jax.sharding import PartitionSpec as P

CG_STEPS = 3


HIGH = lax.Precision.HIGHEST


def apply_system(direction, confidence, fetched, gram):
    low = direction.astype(jnp.bfloat16)
    scores = jnp.einsum("btr,bklr->bktl", low, fetched, preferred_element_type=jnp.float32)
    weighted = (confidence.astype(jnp.float32) * scores).astype(jnp.bfloat16)
    back = jnp.einsum("bktl,bklr->btr", weighted, fetched, preferred_element_type=jnp.float32)
    width = direction.shape[-1]
    global_part = jnp.dot(
        direction.reshape(-1, width), gram, precision=HIGH, preferred_element_type=jnp.float32
    )
    return global_part.reshape(direction.shape) + 0.1 * direction + back


def per_device(lender_block, confidence, lender_factors):
    shards = lax.axis_size("shard")
    blocks, lists = lender_block.shape
    tile = confidence.shape[2]
    rank = lender_factors.shape[1]
    owned = lender_factors.shape[0] // tile
    entries = blocks * lists
    slots = (2 * entries + shards - 1) // shards
    local_gram = lax.dot_general(
        lender_factors, lender_factors, (((0,), (0,)), ((), ())), preferred_element_type=jnp.float32
    )
    gram = lax.psum(local_gram, "shard")
    flat = lender_block.reshape(entries)
    owner = flat // owned
    within = flat - owner * owned
    member = (owner[:, None] == jnp.arange(shards, dtype=jnp.int32)[None, :]).astype(jnp.int32)
    position = jnp.sum(jnp.cumsum(member, axis=0) * member, axis=1) - 1
    slot_index = owner * slots + position
    requests = (
        jnp.zeros((shards * slots,), jnp.int32).at[slot_index].set(within).reshape(shards, slots)
    )
    table = lender_factors.reshape(owned, tile, rank)
    incoming = lax.all_to_all(requests, "shard", split_axis=0, concat_axis=0, tiled=True)
    replies = lax.all_to_all(table[incoming], "shard", split_axis=0, concat_axis=0, tiled=True)
    fetched = replies.reshape(shards * slots, tile, rank)[slot_index].reshape(
        blocks, lists, tile, rank
    )
    rhs = jnp.einsum("bktl,bklr->btr", confidence, fetched, preferred_element_type=jnp.float32)
    solution = jnp.zeros_like(rhs)
    resid = rhs
    direction = rhs
    norm_now = jnp.sum(resid * resid, axis=2, keepdims=True)
    for count in range(CG_STEPS):
        image = apply_system(direction, confidence, fetched, gram)
        alpha = norm_now / (jnp.sum(direction * image, axis=2, keepdims=True) + 1e-06)
        solution = solution + alpha * direction
        resid = resid - alpha * image
        norm_next = jnp.sum(resid * resid, axis=2, keepdims=True)
        direction = resid + norm_next / (norm_now + 1e-06) * direction
        norm_now = norm_next
    solved = solution.astype(jnp.bfloat16)
    partial_rhs = jnp.einsum(
        "bktl,btr->bklr", confidence, solved, preferred_element_type=jnp.float32
    )
    outgoing = (
        jnp.zeros((shards * slots, tile, rank), jnp.float32)
        .at[slot_index]
        .set(partial_rhs.reshape(entries, tile, rank))
    )
    returned = lax.all_to_all(
        outgoing.reshape(shards, slots, tile, rank),
        "shard",
        split_axis=0,
        concat_axis=0,
        tiled=True,
    )
    selector = (
        incoming.reshape(-1)[None, :] == jnp.arange(owned, dtype=jnp.int32)[:, None]
    ).astype(jnp.float32)
    owner_sum = jnp.dot(
        selector,
        returned.reshape(shards * slots, tile * rank),
        precision=HIGH,
        preferred_element_type=jnp.float32,
    )
    total = lax.psum(owner_sum, "rep")
    lenders_all = owned * tile * shards
    lender_rhs = total.reshape(owned * tile, rank) / lenders_all
    return (solution.reshape(blocks * tile, rank), lender_rhs)


def solution(mesh):
    in_specs = (P(("shard", "rep"), None), P(("shard", "rep"), None, None, None), P("shard", None))
    out_specs = (P(("shard", "rep"), None), P("shard", None))
    return jax.shard_map(
        per_device, mesh=mesh, in_specs=in_specs, out_specs=out_specs, check_vma=False
    )
```

profile of v0, /device:TPU:0, one launch (start us, length us, event | category | flops | bytes accessed | tf_op | source)
XLA Modules:
  0.0 416.4 jit_solution(9014133852448018927)
XLA Ops:
  7.2 0.0 copy-start
  7.2 0.9 reshape.224
  8.1 0.8 reshape.223
  8.9 0.1 fusion.50
  9.0 0.2 select_reduce_fusion
  9.2 0.6 scatter_custom_fusion
  9.8 0.1 all_to_all.14
  9.9 13.6 %all_to_all.22 = s32[8,1,6]{2,1,0:T(1,128)S(1)} all-to-all(s32[8,1,6]{2,1,0:T(1,128)S(1)} %bitcast.112), channel_id=1, replica_groups=mesh['shard'=8,'rep'=4] {'shard'}, dimensions={0} | all-to-all | bytes 384 | tf_op jit(solution)/shard_map/all_to_all | solution.py:46
  23.5 0.1 copy.32
  23.6 0.1 copy.33
  23.7 0.1 reshape.233
  23.8 0.0 copy-done
  23.8 2.7 gather_fusion
  26.5 4.4 %all-to-all-start.1 = ((bf16[8,6,256,128]{3,2,1,0:T(8,128)(2,1)}), bf16[8,6,256,128]{3,2,1,0:T(8,128)(2,1)}, u32[]{:S(2)}, u32[]{:S(2)}) async-start(bf16[8,6,256,128]{3,2,1,0:T(8,128)(2,1)} %bitcast.106), calls=%async_computation.1 | async-start | bytes 6291456 | tf_op jit(solution)/shard_map/all_to_all | solution.py:47
  30.9 0.0 all-reduce.3.cloned.1.call-start
  31.0 1.4 fusion.55
  32.4 0.0 all-reduce.3.cloned.1.call-update
  32.4 4.7 %copy.37 = bf16[3,8,256,256]{2,3,1,0:T(8,128)(2,1)} copy(bf16[3,8,256,256]{3,2,1,0:T(8,128)(2,1)} %param.4) | data formatting | bytes 6291456 | tf_op args[1]
  37.1 64.9 %all-to-all-done.1 = bf16[8,6,256,128]{3,2,1,0:T(8,128)(2,1)} async-done(((bf16[8,6,256,128]{3,2,1,0:T(8,128)(2,1)}), bf16[8,6,256,128]{3,2,1,0:T(8,128)(2,1)}, u32[]{:S(2)}, u32[]{:S(2)}) %all-to-all-start.1) | async-done | bytes 3145760 | tf_op jit(solution)/shard_map/all_to_all | solution.py:47
  102.0 3.8 gather_fusion.1
  105.8 3.5 convolution_bitcast_fusion
  109.4 4.3 %fusion.18 = f32[3,256,128]{1,2,0:T(8,128)S(1)} fusion(bf16[3,8,256,128]{3,2,1,0:T(8,128)(2,1)} %bitcast.108, bf16[3,8,256,256]{2,3,1,0:T(8,128)(2,1)} %copy.37, f32[3,256,128]{1,2,0:T(8,128)S(1)} %convolution_bitcast_fusion), kind=kOutput, calls=%fused_computation.20 | convolution fusion | flops 810123264 | bytes 5505024 | tf_op jit(solution)/shard_map/bktl,bklr->btr/dot_general | solution.py:16
  113.7 13.5 %all-reduce.3.cloned.1.call-done = f32[128,128]{1,0:T(8,128)} async-done(((f32[128,128]{1,0:T(8,128)}), f32[128,128]{1,0:T(8,128)}) %all-reduce.3.cloned.1.call-update) | async-done | bytes 65552 | tf_op jit(solution)/shard_map/psum | solution.py:35
  127.2 1.4 multiply_reduce_fusion.3
  128.6 0.1 multiply_reduce_fusion.2
  128.7 0.1 multiply_add_fusion.2
  128.7 0.0 copy-start.2
  128.8 5.1 %fusion.21 = f32[3,256,128]{1,2,0:T(8,128)} fusion(bf16[3,8,256,128]{3,2,1,0:T(8,128)(2,1)} %bitcast.109, bf16[3,8,256,256]{2,3,1,0:T(8,128)(2,1)} %copy.37, f32[3,256,128]{1,2,0:T(8,128)S(1)} %multiply_add_fusion.2), kind=kOutput, calls=%fused_computation.21 | convolution fusion | flops 810123264 | bytes 5505024 | tf_op jit(solution)/shard_map/bktl,bklr->btr/dot_general | solution.py:16
  133.8 0.0 copy-done.2
  133.8 1.6 multiply_reduce_fusion.1
  135.4 0.1 multiply_reduce_fusion
  135.5 0.8 multiply_add_fusion.1
  136.3 0.0 copy-start.1
  136.3 5.2 %fusion.24 = f32[3,256,128]{1,2,0:T(8,128)} fusion(bf16[3,8,256,128]{3,2,1,0:T(8,128)(2,1)} %bitcast.110, bf16[3,8,256,256]{2,3,1,0:T(8,128)(2,1)} %copy.37, f32[3,256,128]{1,2,0:T(8,128)} %multiply_add_fusion.1), kind=kOutput, calls=%fused_computation.22 | convolution fusion | flops 810123264 | bytes 5505024 | tf_op jit(solution)/shard_map/bktl,bklr->btr/dot_general | solution.py:16
  141.5 0.0 copy-done.1
  141.5 1.6 fusion.31
  143.1 1.1 multiply_add_fusion
  144.2 4.1 fusion.38
  148.3 3.6 copy.52
  151.9 3.4 broadcast_in_dim.5
  155.3 7.9 %scatter_fusion = f32[48,256,128]{2,1,0:T(8,128)} fusion(f32[48,256,128]{2,1,0:T(8,128)} %broadcast_in_dim.5, s32[24]{0:T(128)S(1)} %fusion.52, f32[24,256,128]{2,1,0:T(8,128)} %copy.52), kind=kCustom, calls=%fused_computation.3 | custom fusion | bytes 9437280 | tf_op jit(solution)/shard_map/scatter | solution.py:71
  163.2 4.8 %all-to-all-start.2 = ((f32[8,6,256,128]{3,2,1,0:T(8,128)}), f32[8,6,256,128]{3,2,1,0:T(8,128)}, u32[]{:S(2)}, u32[]{:S(2)}) async-start(f32[8,6,256,128]{3,2,1,0:T(8,128)} %bitcast.104), calls=%async_computation.2 | async-start | bytes 12582912 | tf_op jit(solution)/shard_map/all_to_all | solution.py:73
  168.0 0.2 all-reduce.5.cloned.1.call-start
  168.2 0.5 broadcast.206
  168.7 0.7 reduce.3
  169.4 0.1 eq.31
  169.5 135.2 %all-to-all-done.2 = f32[8,6,256,128]{3,2,1,0:T(8,128)} async-done(((f32[8,6,256,128]{3,2,1,0:T(8,128)}), f32[8,6,256,128]{3,2,1,0:T(8,128)}, u32[]{:S(2)}, u32[]{:S(2)}) %all-to-all-start.2) | async-done | bytes 6291488 | tf_op jit(solution)/shard_map/all_to_all | solution.py:73
  304.7 10.8 %fusion.3 = f32[32,32768]{1,0:T(8,128)} fusion(f32[6,8,256,128]{3,2,1,0:T(8,128)} %bitcast.40, s32[48]{0:T(128)S(1)} %eq.31), kind=kOutput, calls=%fused_computation.10 | convolution fusion | flops 603981312 | bytes 10485952 | tf_op jit(solution)/shard_map/dot_general | solution.py:83
  315.5 0.0 all-reduce.5.cloned.1.call-update
  315.6 0.9 copy.51
  316.5 83.8 %all-reduce.5.cloned.1.call-done = f32[32,32768]{1,0:T(8,128)} async-done(((f32[32,32768]{1,0:T(8,128)}), f32[32,32768]{1,0:T(8,128)}) %all-reduce.5.cloned.1.call-update) | async-done | bytes 4194320 | tf_op jit(solution)/shard_map/psum | solution.py:89
  400.3 4.4 %broadcast_multiply_fusion = f32[32,32768]{1,0:T(8,128)} fusion(f32[32,32768]{1,0:T(8,128)} %all-reduce.5.cloned.1.call-done), kind=kLoop, calls=%fused_computation.19 | loop fusion | flops 1048576 | bytes 8388608 | tf_op jit(solution)/shard_map/div | solution.py:91
  404.7 4.9 %div.83 = f32[8192,128]{1,0:T(8,128)} reshape(f32[32,32768]{1,0:T(8,128)} %broadcast_multiply_fusion) | data formatting | bytes 8388608 | tf_op jit(solution)/shard_map/div | solution.py:91
  (11 shorter events, 0.1 us)
Async XLA Ops:
  7.2 16.6 %copy-start = (bf16[8192,128]{1,0:T(8,128)(2,1)S(1)}, bf16[8192,128]{1,0:T(8,128)(2,1)}, u32[]{:S(2)}) copy-start(bf16[8192,128]{1,0:T(8,128)(2,1)} %param.5) | copy-start | bytes 6291460
  26.5 75.5 %all-to-all-start.1 = ((bf16[8,6,256,128]{3,2,1,0:T(8,128)(2,1)}), bf16[8,6,256,128]{3,2,1,0:T(8,128)(2,1)}, u32[]{:S(2)}, u32[]{:S(2)}) async-start(bf16[8,6,256,128]{3,2,1,0:T(8,128)(2,1)} %bitcast.106), calls=%async_computation.1 | async-start | bytes 6291456 | tf_op jit(solution)/shard_map/all_to_all | solution.py:47
  30.9 96.2 %all-reduce.3.cloned.1.call-start = ((), (), s32[]{:S(2)}) async-start(), calls=%async_computation.3 | async-start | bytes 131072 | tf_op jit(solution)/shard_map/psum | solution.py:35
  128.7 5.1 %copy-start.2 = (f32[128,128]{1,0:T(8,128)S(1)}, f32[128,128]{1,0:T(8,128)}, u32[]{:S(2)}) copy-start(f32[128,128]{1,0:T(8,128)} %all-reduce.3.cloned.1.call-done) | copy-start | bytes 196612
  136.3 5.2 %copy-start.1 = (f32[3,256,128]{1,2,0:T(8,128)S(1)}, f32[3,256,128]{1,2,0:T(8,128)}, u32[]{:S(2)}) copy-start(f32[3,256,128]{1,2,0:T(8,128)} %multiply_add_fusion.1) | copy-start | bytes 1179652
  163.2 141.5 %all-to-all-start.2 = ((f32[8,6,256,128]{3,2,1,0:T(8,128)}), f32[8,6,256,128]{3,2,1,0:T(8,128)}, u32[]{:S(2)}, u32[]{:S(2)}) async-start(f32[8,6,256,128]{3,2,1,0:T(8,128)} %bitcast.104), calls=%async_computation.2 | async-start | bytes 12582912 | tf_op jit(solution)/shard_map/all_to_all | solution.py:73
  168.0 232.3 %all-reduce.5.cloned.1.call-start = ((), (), s32[]{:S(2)}) async-start(), calls=%async_computation.4 | async-start | bytes 8388608 | tf_op jit(solution)/shard_map/psum | solution.py:89
Sparse Core Ops, SparseCore 0:
  35.7 91.3 all-reduce.2
  315.7 84.5 all-reduce.4
where the time goes:
time: 417 us; the launch traced here: 416 us
  waiting for transfers between devices  297 us (71%)
  matrix products  39 us (9%)
  local copies, waits for them, and re-layouts  35.2 us (8%)
  between operations  14.2 us (3%)
  blocking collectives  13.6 us (3%)
  starting transfers between devices  9.46 us (2%)
  other arithmetic  7.59 us (2%)
    all_to_all x1, waiting for transfers between devices, per_device(): lax.all_to_all(outgoing.reshape(shards, slots, tile, rank), 'shard', spli...  135 us
    psum x1, waiting for transfers between devices, per_device(): total = lax.psum(owner_sum, 'rep')  83.8 us
    all_to_all x1, waiting for transfers between devices, per_device(): lax.all_to_all(table[incoming], 'shard', split_axis=0, concat_axis=0, til...  64.9 us
    dot_general x3, matrix products, apply_system(): jnp.einsum('bktl,bklr->btr', weighted, fetched, preferred_element_type=jn...  14.5 us
    all_to_all x1, blocking collectives, per_device(): lax.all_to_all(requests, 'shard', split_axis=0, concat_axis=0, tiled=True)  13.6 us
    psum x1, waiting for transfers between devices, per_device(): gram = lax.psum(local_gram, 'shard')  13.5 us
    dot_general x1, matrix products, per_device(): jnp.dot(selector, returned.reshape(shards * slots, tile * rank), precisio...  10.8 us
  transfers between devices with their start and end apart: 4, of which 4 were waited for; matrix products, arithmetic and copies ran while one was open for 5% of the time, Pallas kernels for 0%

commit v1 on v0

--- a/solution.py
+++ b/solution.py
@@ -21,6 +21,27 @@
     return global_part.reshape(direction.shape) + 0.1 * direction + back
 
 
+WIRE = jnp.float16
+TOP = 14.0
+EXTRA = 16
+
+
+def encode(value):
+    largest = jnp.maximum(jnp.max(jnp.abs(value)), 1e-30)
+    level = jnp.ceil(jnp.log2(largest))
+    return (value * jnp.exp2(TOP - level)).astype(WIRE), level
+
+
+def with_level(chunks, level):
+    head = jnp.broadcast_to(level.astype(WIRE), (chunks.shape[0], EXTRA, chunks.shape[2]))
+    return jnp.concatenate([chunks, head], axis=1)
+
+
+def decode(packed, rows):
+    level = packed[:, rows : rows + 1, :1].astype(jnp.float32)
+    return packed[:, :rows].astype(jnp.float32) * jnp.exp2(level - TOP)
+
+
 def per_device(lender_block, confidence, lender_factors):
     shards = lax.axis_size("shard")
     blocks, lists = lender_block.shape
@@ -29,22 +50,32 @@
     owned = lender_factors.shape[0] // tile
     entries = blocks * lists
     slots = (2 * entries + shards - 1) // shards
+    reps = lax.axis_size("rep")
+    me = lax.axis_index("shard")
+    part = tile // reps
     local_gram = lax.dot_general(
         lender_factors, lender_factors, (((0,), (0,)), ((), ())), preferred_element_type=jnp.float32
     )
-    gram = lax.psum(local_gram, "shard")
     flat = lender_block.reshape(entries)
+    listed = lax.all_gather(flat, ("shard", "rep"), axis=0, tiled=False)
+    mine = (listed // owned == me).astype(jnp.int32)
+    place = jnp.cumsum(mine, axis=1) - 1
+    slot_ids = jnp.arange(slots, dtype=jnp.int32)
+    hit = (place[:, :, None] == slot_ids) & (mine[:, :, None] == 1)
+    within = listed - owned * me
+    named = jnp.sum(jnp.where(hit, within[:, :, None] + 1, 0), axis=1) - 1
     owner = flat // owned
-    within = flat - owner * owned
     member = (owner[:, None] == jnp.arange(shards, dtype=jnp.int32)[None, :]).astype(jnp.int32)
     position = jnp.sum(jnp.cumsum(member, axis=0) * member, axis=1) - 1
     slot_index = owner * slots + position
-    requests = (
-        jnp.zeros((shards * slots,), jnp.int32).at[slot_index].set(within).reshape(shards, slots)
+    table = lender_factors.reshape(owned, tile, rank)
+    incoming = lax.dynamic_index_in_dim(
+        named.reshape(shards, reps, slots), lax.axis_index("rep"), axis=1, keepdims=False
     )
-    table = lender_factors.reshape(owned, tile, rank)
-    incoming = lax.all_to_all(requests, "shard", split_axis=0, concat_axis=0, tiled=True)
-    replies = lax.all_to_all(table[incoming], "shard", split_axis=0, concat_axis=0, tiled=True)
+    wanted = table[jnp.maximum(incoming, 0)]
+    wanted, local_gram = lax.optimization_barrier((wanted, local_gram))
+    gram = lax.psum(local_gram, "shard")
+    replies = lax.all_to_all(wanted, "shard", split_axis=0, concat_axis=0, tiled=True)
     fetched = replies.reshape(shards * slots, tile, rank)[slot_index].reshape(
         blocks, lists, tile, rank
     )
@@ -65,30 +96,31 @@
     partial_rhs = jnp.einsum(
         "bktl,btr->bklr", confidence, solved, preferred_element_type=jnp.float32
     )
-    outgoing = (
-        jnp.zeros((shards * slots, tile, rank), jnp.float32)
-        .at[slot_index]
-        .set(partial_rhs.reshape(entries, tile, rank))
-    )
-    returned = lax.all_to_all(
-        outgoing.reshape(shards, slots, tile, rank),
-        "shard",
-        split_axis=0,
-        concat_axis=0,
-        tiled=True,
-    )
+    coded, level = encode(partial_rhs)
+    every = jnp.arange(shards * slots, dtype=jnp.int32)
+    source = jnp.argmax(slot_index[None, :] == every[:, None], axis=1).astype(jnp.int32)
+    quarter = jnp.arange(reps, dtype=jnp.int32)
+    pick = source.reshape(shards, 1, slots) * reps + quarter[None, :, None]
+    chunks = coded.reshape(entries * reps, part, rank)[pick.reshape(-1)]
+    chunks = chunks.reshape(shards * reps, slots * part, rank)
+    outgoing = with_level(chunks, level)
+    returned = lax.all_to_all(outgoing, ("shard", "rep"), split_axis=0, concat_axis=0, tiled=True)
+    back = decode(returned, slots * part)
     selector = (
-        incoming.reshape(-1)[None, :] == jnp.arange(owned, dtype=jnp.int32)[:, None]
+        named.reshape(-1)[None, :] == jnp.arange(owned, dtype=jnp.int32)[:, None]
     ).astype(jnp.float32)
     owner_sum = jnp.dot(
         selector,
-        returned.reshape(shards * slots, tile * rank),
+        back.reshape(shards * reps * slots, part * rank),
         precision=HIGH,
         preferred_element_type=jnp.float32,
     )
-    total = lax.psum(owner_sum, "rep")
+    coded, level = encode(owner_sum.reshape(owned * part, rank))
+    shared = lax.all_gather(with_level(coded[None], level)[0], "rep", axis=0, tiled=False)
     lenders_all = owned * tile * shards
-    lender_rhs = total.reshape(owned * tile, rank) / lenders_all
+    total = decode(shared, owned * part) / lenders_all
+    lender_rhs = total.reshape(reps, owned, part, rank).transpose(1, 0, 2, 3)
+    lender_rhs = lender_rhs.reshape(owned * tile, rank)
     return (solution.reshape(blocks * tile, rank), lender_rhs)
 
 

time: 417 us -> 332 us (0.80)
  waiting for transfers between devices: 297 us -> 160 us
  blocking collectives: 13.6 us -> 58.7 us
  other arithmetic: 7.59 us -> 13.7 us
  matrix products: 39 us -> 34.7 us
    psum x1 -> x0, waiting for transfers between devices: 83.8 us -> none  [per_device(): total = lax.psum(owner_sum, 'rep')]
    all_to_all x2, waiting for transfers between devices: 200 us -> 139 us  [the longest x1 73.1 us: per_device(): lax.all_to_all(outgoing, ('shard', 'rep'), split_axis=0, concat_axis=0, t...]
    all_gather x0 -> x2, blocking collectives: none -> 58.7 us  [the longest x1 43.3 us: per_device(): listed = lax.all_gather(flat, ('shard', 'rep'), axis=0, tiled=False)]
    all_to_all x1 -> x0, blocking collectives: 13.6 us -> none  [per_device(): lax.all_to_all(requests, 'shard', split_axis=0, concat_axis=0, tiled=True)]
    scatter x2 -> x0, local copies, waits for them, and re-layouts: 8.56 us -> none  [the longest x1 7.91 us: per_device(): outgoing = jnp.zeros((shards * slots, tile, rank), jnp.float32).at[slot_i...]
    psum x1, waiting for transfers between devices: 13.5 us -> 20.3 us  [per_device(): gram = lax.psum(local_gram, 'shard')]
    mul x0 -> x3, other arithmetic: none -> 5.34 us  [the longest x2 5.34 us: decode(): return packed[:, :rows].astype(jnp.float32) * jnp.exp2(level - TOP)]
    dot_general x1, matrix products: 10.8 us -> 5.95 us  [per_device(): jnp.dot(selector, back.reshape(shards * reps * slots, part * rank), preci...]
  transfers between devices with their start and end apart: 4 -> 3, of which waited for: 4 -> 3; matrix products, arithmetic and copies ran while one was open for 5% -> 6% of each run, Pallas kernels for 0% -> 0%
where the time goes in v1:
time: 332 us; the launch traced here: 331 us
  waiting for transfers between devices  160 us (48%)
  blocking collectives  58.7 us (18%)
  local copies, waits for them, and re-layouts  38.1 us (11%)
  matrix products  34.7 us (10%)
  between operations  15.7 us (5%)
  other arithmetic  13.7 us (4%)
  starting transfers between devices  9.45 us (3%)
    all_to_all x1, waiting for transfers between devices, per_device(): lax.all_to_all(outgoing, ('shard', 'rep'), split_axis=0, concat_axis=0, t...  73.1 us
    all_to_all x1, waiting for transfers between devices, per_device(): lax.all_to_all(wanted, 'shard', split_axis=0, concat_axis=0, tiled=True)  66.2 us
    all_gather x1, blocking collectives, per_device(): listed = lax.all_gather(flat, ('shard', 'rep'), axis=0, tiled=False)  43.3 us
    psum x1, waiting for transfers between devices, per_device(): gram = lax.psum(local_gram, 'shard')  20.3 us
    all_gather x1, blocking collectives, per_device(): lax.all_gather(with_level(coded[None], level)[0], 'rep', axis=0, tiled=Fa...  15.4 us
    dot_general x3, matrix products, apply_system(): jnp.einsum('bktl,bklr->btr', weighted, fetched, preferred_element_type=jn...  14.5 us
    reshape x1, local copies, waits for them, and re-layouts, per_device(): back.reshape(shards * reps * slots, part * rank)  7.15 us
  transfers between devices with their start and end apart: 3, of which 3 were waited for; matrix products, arithmetic and copies ran while one was open for 6% of the time, Pallas kernels for 0%

profile of v1, /device:TPU:0, one launch (start us, length us, event | category | flops | bytes accessed | tf_op | source)
XLA Modules:
  0.0 330.6 jit_solution(16797563167929177055)
XLA Ops:
  7.2 0.0 copy-start
  7.2 0.9 reshape.352
  8.1 43.3 %all-gather = s32[32,1,24]{2,1,0:T(1,128)S(1)} all-gather(s32[1,1,24]{2,1,0:T(1,128)S(1)} %reshape.352), channel_id=1, replica_groups=mesh['shard'=8,'rep'=4] {'shard','rep'}, dimensions={0}, use_global_device_ids=true | all-gather | bytes 3168 | tf_op jit(solution)/shard_map/all_gather | solution.py:60
  51.4 0.1 copy.157
  51.5 0.1 copy.156
  51.6 0.2 reduce_window_sum.22
  51.7 0.1 copy.155
  51.9 0.1 sub.59
  51.9 0.1 dynamic-slice_maximum_fusion
  52.0 0.1 copy.158
  52.2 0.1 reshape.328
  52.3 0.0 copy-done
  52.3 1.4 fusion.62
  53.7 2.7 gather_fusion
  56.4 4.6 %all-to-all-start = ((bf16[8,6,256,128]{3,2,1,0:T(8,128)(2,1)}), bf16[8,6,256,128]{3,2,1,0:T(8,128)(2,1)}, u32[]{:S(2)}, u32[]{:S(2)}) async-start(bf16[8,6,256,128]{3,2,1,0:T(8,128)(2,1)} %bitcast.109), calls=%async_computation | async-start | bytes 6291456 | tf_op jit(solution)/shard_map/all_to_all | solution.py:78
  60.9 0.0 all-reduce.4.cloned.1.call-start
  61.0 0.7 all-reduce.4.cloned.1.call-update
  61.7 0.0 copy-done.3
  61.7 0.1 reshape.318
  61.8 0.1 reshape.317
  61.9 0.1 fusion.55
  62.0 0.2 select_reduce_fusion.1
  62.2 0.6 iota_reduce_fusion
  62.8 0.1 mul.197
  62.9 0.1 add.216
  63.0 4.7 %copy.162 = bf16[3,8,256,256]{2,3,1,0:T(8,128)(2,1)} copy(bf16[3,8,256,256]{3,2,1,0:T(8,128)(2,1)} %param.4) | data formatting | bytes 6291456 | tf_op args[1]
  67.7 66.2 %all-to-all-done = bf16[8,6,256,128]{3,2,1,0:T(8,128)(2,1)} async-done(((bf16[8,6,256,128]{3,2,1,0:T(8,128)(2,1)}), bf16[8,6,256,128]{3,2,1,0:T(8,128)(2,1)}, u32[]{:S(2)}, u32[]{:S(2)}) %all-to-all-start) | async-done | bytes 3145760 | tf_op jit(solution)/shard_map/all_to_all | solution.py:78
  133.9 3.8 %gather_fusion.1 = bf16[24,256,128]{2,1,0:T(8,128)(2,1)} fusion(bf16[48,256,128]{2,1,0:T(8,128)(2,1)} %bitcast.3, s32[1024]{0:T(1024)S(1)} %pad_clamp_fusion.1), kind=kCustom, calls=%fused_computation.1 | custom fusion | bytes 3145824 | tf_op jit(solution)/shard_map/gather | solution.py:79
  137.7 3.5 %convolution_bitcast_fusion = f32[3,256,128]{1,2,0:T(8,128)S(1)} fusion(bf16[3,8,256,128]{3,2,1,0:T(8,128)(2,1)} %bitcast.111, bf16[3,8,256,256]{3,2,1,0:T(8,128)(2,1)} %param.4), kind=kOutput, calls=%fused_computation.26 | convolution fusion | flops 402653184 | bytes 5111808 | tf_op jit(solution)/shard_map/bktl,bklr->btr/dot_general | solution.py:82
  141.3 4.3 %fusion.16 = f32[3,256,128]{1,2,0:T(8,128)S(1)} fusion(bf16[3,8,256,128]{3,2,1,0:T(8,128)(2,1)} %bitcast.112, bf16[3,8,256,256]{2,3,1,0:T(8,128)(2,1)} %copy.162, f32[3,256,128]{1,2,0:T(8,128)S(1)} %convolution_bitcast_fusion), kind=kOutput, calls=%fused_computation.20 | convolution fusion | flops 810123264 | bytes 5505024 | tf_op jit(solution)/shard_map/bktl,bklr->btr/dot_general | solution.py:16
  145.6 20.3 %all-reduce.4.cloned.1.call-done = f32[128,128]{1,0:T(8,128)} async-done(((f32[128,128]{1,0:T(8,128)}), f32[128,128]{1,0:T(8,128)}) %all-reduce.4.cloned.1.call-update) | async-done | bytes 65552 | tf_op jit(solution)/shard_map/psum | solution.py:77
  165.9 1.4 multiply_reduce_fusion.3
  167.3 0.1 multiply_reduce_fusion.2
  167.4 0.1 multiply_add_fusion.2
  167.5 0.0 copy-start.2
  167.5 5.1 %fusion.19 = f32[3,256,128]{1,2,0:T(8,128)} fusion(bf16[3,8,256,128]{3,2,1,0:T(8,128)(2,1)} %bitcast.113, bf16[3,8,256,256]{2,3,1,0:T(8,128)(2,1)} %copy.162, f32[3,256,128]{1,2,0:T(8,128)S(1)} %multiply_add_fusion.2), kind=kOutput, calls=%fused_computation.21 | convolution fusion | flops 810123264 | bytes 5505024 | tf_op jit(solution)/shard_map/bktl,bklr->btr/dot_general | solution.py:16
  172.6 1.6 multiply_reduce_fusion.1
  174.1 0.1 multiply_reduce_fusion
  174.2 0.8 multiply_add_fusion.1
  175.1 5.2 %fusion.22 = f32[3,256,128]{1,2,0:T(8,128)} fusion(bf16[3,8,256,128]{3,2,1,0:T(8,128)(2,1)} %bitcast.114, bf16[3,8,256,256]{2,3,1,0:T(8,128)(2,1)} %copy.162, f32[3,256,128]{1,2,0:T(8,128)} %multiply_add_fusion.1), kind=kOutput, calls=%fused_computation.22 | convolution fusion | flops 810123264 | bytes 5505024 | tf_op jit(solution)/shard_map/bktl,bklr->btr/dot_general | solution.py:16
  180.2 1.6 fusion.29
  181.8 1.1 multiply_add_fusion
  182.9 4.7 %abs_reduce_fusion = (f32[]{:T(128)}, f32[3,128,8,256]{3,1,2,0:T(8,128)}) fusion(bf16[3,8,256,256]{3,2,1,0:T(8,128)(2,1)} %param.4, f32[3,256,128]{1,2,0:T(8,128)S(1)} %multiply_add_fusion), kind=kOutput, calls=%fused_computation.15 | convolution fusion | flops 404324352 | bytes 6684676 | tf_op jit(solution)/shard_map/bktl,btr->bklr/dot_general | solution.py:96
  188.4 3.5 %fusion.15 = f16[3,8,256,128]{2,3,1,0:T(8,128)(2,1)} fusion(f32[3,128,8,256]{3,1,2,0:T(8,128)} %get-tuple-element.18, f32[]{:T(128)S(6)} %exp2.28), kind=kLoop, calls=%fused_computation.19 | loop fusion | flops 1572864 | bytes 4718596 | tf_op jit(solution)/shard_map/convert_element_type | solution.py:32
  191.9 3.0 copy.178
  194.9 4.8 %gather_fusion.2 = f16[192,64,128]{2,1,0:T(8,128)(2,1)} fusion(f16[96,64,128]{2,1,0:T(8,128)(2,1)} %bitcast.108, s32[1024]{0:T(1024)S(1)} %pad_clamp_fusion), kind=kCustom, calls=%fused_computation.2 | custom fusion | bytes 6292224 | tf_op jit(solution)/shard_map/gather | solution.py:104
  199.7 4.2 %concatenate.6 = f16[32,400,128]{2,1,0:T(8,128)(2,1)} pad(f16[32,384,128]{2,1,0:T(8,128)(2,1)} %bitcast.110, f16[]{:T(256)S(6)} %convert_element_type.82), padding=0_0x0_16x0_0 | pad | bytes 6422530 | tf_op jit(solution)/shard_map/concatenate | solution.py:37
  203.9 4.8 %all-to-all-start.1 = ((f16[32,400,128]{2,1,0:T(8,128)(2,1)}), f16[32,400,128]{2,1,0:T(8,128)(2,1)}, u32[]{:S(2)}, u32[]{:S(2)}) async-start(f16[32,400,128]{2,1,0:T(8,128)(2,1)} %concatenate.6), calls=%async_computation.1 | async-start | bytes 6553600 | tf_op jit(solution)/shard_map/all_to_all | solution.py:107
  208.8 0.1 copy.177
  208.8 0.1 sub.66
  208.9 0.9 copy.176
  209.9 73.1 %all-to-all-done.1 = f16[32,400,128]{2,1,0:T(8,128)(2,1)} async-done(((f16[32,400,128]{2,1,0:T(8,128)(2,1)}), f16[32,400,128]{2,1,0:T(8,128)(2,1)}, u32[]{:S(2)}, u32[]{:S(2)}) %all-to-all-start.1) | async-done | bytes 3276832 | tf_op jit(solution)/shard_map/all_to_all | solution.py:107
  283.0 0.9 slice.23
  283.9 0.1 copy.209
  284.0 5.3 %convert_multiply_fusion.3 = f32[32,384,128]{2,1,0:T(8,128)} fusion(f16[32,400,128]{2,1,0:T(8,128)(2,1)} %all-to-all-done.1, f32[32]{0:T(128)S(1)} %exponential_bitcast_fusion), kind=kLoop, calls=%fused_computation.9 | loop fusion | flops 3145728 | bytes 9437312 | tf_op jit(solution)/shard_map/mul | solution.py:42
  289.3 7.2 %reshape.323 = f32[192,8192]{1,0:T(8,128)} reshape(f32[32,384,128]{2,1,0:T(8,128)} %convert_multiply_fusion.3) | data formatting | bytes 12582912 | tf_op jit(solution)/shard_map/reshape | solution.py:114
  296.4 5.9 %abs_reduce_fusion.1 = (f32[]{:T(128)}, f32[32,8192]{1,0:T(8,128)S(1)}) fusion(f32[192,8192]{1,0:T(8,128)} %reshape.323, s32[192]{0:T(256)S(1)} %sub.66), kind=kOutput, calls=%fused_computation.33 | convolution fusion | flops 604510208 | bytes 7340804 | tf_op jit(solution)/shard_map/dot_general | solution.py:112
  303.1 0.9 multiply_convert_fusion.1
  304.0 1.3 convert_element_type.86
  305.3 0.1 concatenate.7
  305.5 15.4 %all-gather.2 = f16[4,2064,128]{2,1,0:T(8,128)(2,1)S(1)} all-gather(f16[1,2064,128]{2,1,0:T(8,128)(2,1)S(1)} %concatenate.7), channel_id=1, replica_groups=mesh['shard'=8,'rep'=4] {'rep'}, dimensions={0}, use_global_device_ids=true | all-gather | bytes 2641920 | tf_op jit(solution)/shard_map/all_gather | solution.py:119
  320.9 0.1 fusion.59
  321.0 0.5 multiply_multiply_fusion
  321.5 2.3 copy.180
  (25 shorter events, 0.3 us)
Async XLA Ops:
  7.2 45.1 %copy-start = (bf16[8192,128]{1,0:T(8,128)(2,1)S(1)}, bf16[8192,128]{1,0:T(8,128)(2,1)}, u32[]{:S(2)}) copy-start(bf16[8192,128]{1,0:T(8,128)(2,1)} %param.5) | copy-start | bytes 6291460
  56.4 5.3 %copy-start.3 = (s32[3,8]{1,0:T(4,128)S(1)}, s32[3,8]{1,0:T(4,128)}, u32[]{:S(2)}) copy-start(s32[3,8]{1,0:T(4,128)} %param.3) | copy-start | bytes 292
  56.4 77.5 %all-to-all-start = ((bf16[8,6,256,128]{3,2,1,0:T(8,128)(2,1)}), bf16[8,6,256,128]{3,2,1,0:T(8,128)(2,1)}, u32[]{:S(2)}, u32[]{:S(2)}) async-start(bf16[8,6,256,128]{3,2,1,0:T(8,128)(2,1)} %bitcast.109), calls=%async_computation | async-start | bytes 6291456 | tf_op jit(solution)/shard_map/all_to_all | solution.py:78
  60.9 104.9 %all-reduce.4.cloned.1.call-start = ((), (), s32[]{:S(2)}) async-start(), calls=%async_computation.2 | async-start | bytes 131072 | tf_op jit(solution)/shard_map/psum | solution.py:77
  167.5 5.1 %copy-start.2 = (f32[128,128]{1,0:T(8,128)S(1)}, f32[128,128]{1,0:T(8,128)}, u32[]{:S(2)}) copy-start(f32[128,128]{1,0:T(8,128)} %all-reduce.4.cloned.1.call-done) | copy-start | bytes 196612
  175.1 5.2 %copy-start.1 = (f32[3,256,128]{1,2,0:T(8,128)S(1)}, f32[3,256,128]{1,2,0:T(8,128)}, u32[]{:S(2)}) copy-start(f32[3,256,128]{1,2,0:T(8,128)} %multiply_add_fusion.1) | copy-start | bytes 1179652
  203.9 79.1 %all-to-all-start.1 = ((f16[32,400,128]{2,1,0:T(8,128)(2,1)}), f16[32,400,128]{2,1,0:T(8,128)(2,1)}, u32[]{:S(2)}, u32[]{:S(2)}) async-start(f16[32,400,128]{2,1,0:T(8,128)(2,1)} %concatenate.6), calls=%async_computation.1 | async-start | bytes 6553600 | tf_op jit(solution)/shard_map/all_to_all | solution.py:107
Sparse Core Ops, SparseCore 0:
  65.7 100.0 all-reduce.3

commit v2 on v1

--- a/solution.py
+++ b/solution.py
@@ -51,29 +51,33 @@
     entries = blocks * lists
     slots = (2 * entries + shards - 1) // shards
     reps = lax.axis_size("rep")
-    me = lax.axis_index("shard")
     part = tile // reps
     local_gram = lax.dot_general(
         lender_factors, lender_factors, (((0,), (0,)), ((), ())), preferred_element_type=jnp.float32
     )
     flat = lender_block.reshape(entries)
-    listed = lax.all_gather(flat, ("shard", "rep"), axis=0, tiled=False)
-    mine = (listed // owned == me).astype(jnp.int32)
-    place = jnp.cumsum(mine, axis=1) - 1
-    slot_ids = jnp.arange(slots, dtype=jnp.int32)
-    hit = (place[:, :, None] == slot_ids) & (mine[:, :, None] == 1)
-    within = listed - owned * me
-    named = jnp.sum(jnp.where(hit, within[:, :, None] + 1, 0), axis=1) - 1
     owner = flat // owned
     member = (owner[:, None] == jnp.arange(shards, dtype=jnp.int32)[None, :]).astype(jnp.int32)
     position = jnp.sum(jnp.cumsum(member, axis=0) * member, axis=1) - 1
     slot_index = owner * slots + position
+    every = jnp.arange(shards * slots, dtype=jnp.int32)
+    match = slot_index[None, :] == every[:, None]
+    within = flat - owner * owned
+    requests = jnp.sum(jnp.where(match, within[None, :] + 1, 0), axis=1) - 1
+    requests = jnp.broadcast_to(requests.reshape(shards, 1, slots), (shards, reps, slots))
+    named = lax.all_to_all(
+        requests.reshape(shards * reps, slots),
+        ("shard", "rep"),
+        split_axis=0,
+        concat_axis=0,
+        tiled=True,
+    )
     table = lender_factors.reshape(owned, tile, rank)
     incoming = lax.dynamic_index_in_dim(
         named.reshape(shards, reps, slots), lax.axis_index("rep"), axis=1, keepdims=False
     )
-    wanted = table[jnp.maximum(incoming, 0)]
-    wanted, local_gram = lax.optimization_barrier((wanted, local_gram))
+    after_gram = (local_gram[0, 0] < 0).astype(jnp.int32)
+    wanted = table[jnp.maximum(incoming, 0) + after_gram]
     gram = lax.psum(local_gram, "shard")
     replies = lax.all_to_all(wanted, "shard", split_axis=0, concat_axis=0, tiled=True)
     fetched = replies.reshape(shards * slots, tile, rank)[slot_index].reshape(
@@ -97,8 +101,7 @@
         "bktl,btr->bklr", confidence, solved, preferred_element_type=jnp.float32
     )
     coded, level = encode(partial_rhs)
-    every = jnp.arange(shards * slots, dtype=jnp.int32)
-    source = jnp.argmax(slot_index[None, :] == every[:, None], axis=1).astype(jnp.int32)
+    source = jnp.argmax(match, axis=1).astype(jnp.int32)
     quarter = jnp.arange(reps, dtype=jnp.int32)
     pick = source.reshape(shards, 1, slots) * reps + quarter[None, :, None]
     chunks = coded.reshape(entries * reps, part, rank)[pick.reshape(-1)]

time: 332 us -> 295 us (0.89)
  blocking collectives: 58.7 us -> 15.4 us
  starting transfers between devices: 9.45 us -> 16.8 us
    all_gather x1 -> x0, blocking collectives: 43.3 us -> none  [per_device(): listed = lax.all_gather(flat, ('shard', 'rep'), axis=0, tiled=False)]
    all_to_all x0 -> x1, starting transfers between devices: none -> 7.33 us  [per_device(): lax.all_to_all(requests.reshape(shards * reps, slots), ('shard', 'rep'),...]
    psum x1, waiting for transfers between devices: 20.3 us -> 13.9 us  [per_device(): gram = lax.psum(local_gram, 'shard')]
    all_to_all x0 -> x1, waiting for transfers between devices: none -> 5.03 us  [per_device(): lax.all_to_all(requests.reshape(shards * reps, slots), ('shard', 'rep'),...]
  transfers between devices with their start and end apart: 3 -> 4, of which waited for: 3 -> 4; matrix products, arithmetic and copies ran while one was open for 6% -> 7% of each run, Pallas kernels for 0% -> 0%
where the time goes in v2:
time: 295 us; the launch traced here: 294 us
  waiting for transfers between devices  158 us (54%)
  local copies, waits for them, and re-layouts  39.5 us (13%)
  matrix products  34.1 us (12%)
  starting transfers between devices  16.8 us (6%)
  between operations  16.5 us (6%)
  blocking collectives  15.4 us (5%)
  other arithmetic  14.4 us (5%)
    all_to_all x1, waiting for transfers between devices, per_device(): lax.all_to_all(outgoing, ('shard', 'rep'), split_axis=0, concat_axis=0, t...  72 us
    all_to_all x1, waiting for transfers between devices, per_device(): lax.all_to_all(wanted, 'shard', split_axis=0, concat_axis=0, tiled=True)  66.1 us
    all_gather x1, blocking collectives, per_device(): lax.all_gather(with_level(coded[None], level)[0], 'rep', axis=0, tiled=Fa...  15.4 us
    dot_general x3, matrix products, apply_system(): jnp.einsum('bktl,bklr->btr', weighted, fetched, preferred_element_type=jn...  14.5 us
    psum x1, waiting for transfers between devices, per_device(): gram = lax.psum(local_gram, 'shard')  13.9 us
    all_to_all x1, starting transfers between devices, per_device(): lax.all_to_all(requests.reshape(shards * reps, slots), ('shard', 'rep'),...  7.33 us
    reshape x1, local copies, waits for them, and re-layouts, per_device(): back.reshape(shards * reps * slots, part * rank)  7.15 us
    dot_general x1, matrix products, per_device(): jnp.dot(selector, back.reshape(shards * reps * slots, part * rank), preci...  5.94 us
  transfers between devices with their start and end apart: 4, of which 4 were waited for; matrix products, arithmetic and copies ran while one was open for 7% of the time, Pallas kernels for 0%

profile of v2, /device:TPU:0, one launch (start us, length us, event | category | flops | bytes accessed | tf_op | source)
XLA Modules:
  0.0 294.4 jit_solution(8399168276270586555)
XLA Ops:
  7.2 0.0 copy-start
  7.2 0.9 reshape.346
  8.1 0.1 fusion.50
  8.2 0.2 select_reduce_fusion.1
  8.4 0.1 select_reduce_fusion
  8.5 0.1 sub.47
  8.6 0.6 broadcast_in_dim.16
  9.2 7.3 %all-to-all-start = ((s32[32,1,6]{2,1,0:T(1,128)}), s32[32,1,6]{2,1,0:T(1,128)S(1)}, u32[]{:S(2)}, u32[]{:S(2)}) async-start(s32[32,1,6]{2,1,0:T(1,128)} %bitcast.1), calls=%async_computation | async-start | bytes 32768 | tf_op jit(solution)/shard_map/all_to_all | solution.py:68
  16.6 0.0 copy-done
  16.6 0.7 fusion.56
  17.3 0.0 copy-start.3
  17.3 0.6 slice.26
  18.6 5.0 %all-to-all-done = s32[32,1,6]{2,1,0:T(1,128)S(1)} async-done(((s32[32,1,6]{2,1,0:T(1,128)}), s32[32,1,6]{2,1,0:T(1,128)S(1)}, u32[]{:S(2)}, u32[]{:S(2)}) %all-to-all-start) | async-done | bytes 800 | tf_op jit(solution)/shard_map/all_to_all | solution.py:68
  23.7 0.1 copy.199
  23.8 0.2 add_reduce_fusion
  24.0 0.1 copy.148
  24.1 0.1 reshape.360
  24.2 2.7 gather_fusion
  26.9 4.6 %all-to-all-start.1 = ((bf16[8,6,256,128]{3,2,1,0:T(8,128)(2,1)}), bf16[8,6,256,128]{3,2,1,0:T(8,128)(2,1)}, u32[]{:S(2)}, u32[]{:S(2)}) async-start(bf16[8,6,256,128]{3,2,1,0:T(8,128)(2,1)} %bitcast.110), calls=%async_computation.1 | async-start | bytes 6291456 | tf_op jit(solution)/shard_map/all_to_all | solution.py:82
  31.5 0.0 all-reduce.4.cloned.1.call-start
  31.5 0.7 all-reduce.4.cloned.1.call-update
  32.2 0.1 reshape.349
  32.3 0.6 iota_reduce_fusion
  32.9 0.1 mul.201
  33.0 0.1 add.247
  33.1 4.7 %copy.152 = bf16[3,8,256,256]{2,3,1,0:T(8,128)(2,1)} copy(bf16[3,8,256,256]{3,2,1,0:T(8,128)(2,1)} %param.4) | data formatting | bytes 6291456 | tf_op args[1]
  37.8 66.1 %all-to-all-done.1 = bf16[8,6,256,128]{3,2,1,0:T(8,128)(2,1)} async-done(((bf16[8,6,256,128]{3,2,1,0:T(8,128)(2,1)}), bf16[8,6,256,128]{3,2,1,0:T(8,128)(2,1)}, u32[]{:S(2)}, u32[]{:S(2)}) %all-to-all-start.1) | async-done | bytes 3145760 | tf_op jit(solution)/shard_map/all_to_all | solution.py:82
  104.0 3.8 %gather_fusion.1 = bf16[24,256,128]{2,1,0:T(8,128)(2,1)} fusion(bf16[48,256,128]{2,1,0:T(8,128)(2,1)} %bitcast.5, s32[1024]{0:T(1024)S(1)} %pad_clamp_fusion.1), kind=kCustom, calls=%fused_computation.1 | custom fusion | bytes 3145824 | tf_op jit(solution)/shard_map/gather | solution.py:83
  107.8 3.5 %convolution_bitcast_fusion = f32[3,256,128]{1,2,0:T(8,128)S(1)} fusion(bf16[3,8,256,128]{3,2,1,0:T(8,128)(2,1)} %bitcast.112, bf16[3,8,256,256]{3,2,1,0:T(8,128)(2,1)} %param.4), kind=kOutput, calls=%fused_computation.26 | convolution fusion | flops 402653184 | bytes 5111808 | tf_op jit(solution)/shard_map/bktl,bklr->btr/dot_general | solution.py:86
  111.4 4.3 %fusion.16 = f32[3,256,128]{1,2,0:T(8,128)S(1)} fusion(bf16[3,8,256,128]{3,2,1,0:T(8,128)(2,1)} %bitcast.113, bf16[3,8,256,256]{2,3,1,0:T(8,128)(2,1)} %copy.152, f32[3,256,128]{1,2,0:T(8,128)S(1)} %convolution_bitcast_fusion), kind=kOutput, calls=%fused_computation.20 | convolution fusion | flops 810123264 | bytes 5505024 | tf_op jit(solution)/shard_map/bktl,bklr->btr/dot_general | solution.py:16
  115.7 13.9 %all-reduce.4.cloned.1.call-done = f32[128,128]{1,0:T(8,128)} async-done(((f32[128,128]{1,0:T(8,128)}), f32[128,128]{1,0:T(8,128)}) %all-reduce.4.cloned.1.call-update) | async-done | bytes 65552 | tf_op jit(solution)/shard_map/psum | solution.py:81
  129.6 1.4 multiply_reduce_fusion.3
  131.0 0.1 multiply_reduce_fusion.2
  131.1 0.1 multiply_add_fusion.2
  131.2 5.1 %fusion.19 = f32[3,256,128]{1,2,0:T(8,128)} fusion(bf16[3,8,256,128]{3,2,1,0:T(8,128)(2,1)} %bitcast.114, bf16[3,8,256,256]{2,3,1,0:T(8,128)(2,1)} %copy.152, f32[3,256,128]{1,2,0:T(8,128)S(1)} %multiply_add_fusion.2), kind=kOutput, calls=%fused_computation.21 | convolution fusion | flops 810123264 | bytes 5505024 | tf_op jit(solution)/shard_map/bktl,bklr->btr/dot_general | solution.py:16
  136.3 1.6 multiply_reduce_fusion.1
  137.8 0.1 multiply_reduce_fusion
  137.9 0.8 multiply_add_fusion.1
  138.8 5.2 %fusion.22 = f32[3,256,128]{1,2,0:T(8,128)} fusion(bf16[3,8,256,128]{3,2,1,0:T(8,128)(2,1)} %bitcast.115, bf16[3,8,256,256]{2,3,1,0:T(8,128)(2,1)} %copy.152, f32[3,256,128]{1,2,0:T(8,128)} %multiply_add_fusion.1), kind=kOutput, calls=%fused_computation.22 | convolution fusion | flops 810123264 | bytes 5505024 | tf_op jit(solution)/shard_map/bktl,bklr->btr/dot_general | solution.py:16
  144.0 1.6 fusion.29
  145.5 1.1 multiply_add_fusion
  146.6 4.8 %abs_reduce_fusion = (f32[]{:T(128)}, f32[3,128,8,256]{3,1,2,0:T(8,128)}) fusion(bf16[3,8,256,256]{3,2,1,0:T(8,128)(2,1)} %param.4, f32[3,256,128]{1,2,0:T(8,128)S(1)} %multiply_add_fusion), kind=kOutput, calls=%fused_computation.15 | convolution fusion | flops 404324352 | bytes 6684676 | tf_op jit(solution)/shard_map/bktl,btr->bklr/dot_general | solution.py:100
  152.1 3.5 %fusion.15 = f16[3,8,256,128]{2,3,1,0:T(8,128)(2,1)} fusion(f32[3,128,8,256]{3,1,2,0:T(8,128)} %get-tuple-element.14, f32[]{:T(128)S(6)} %exp2.28), kind=kLoop, calls=%fused_computation.19 | loop fusion | flops 1572864 | bytes 4718596 | tf_op jit(solution)/shard_map/convert_element_type | solution.py:32
  155.6 3.0 %copy.167 = f16[3,8,256,128]{3,2,1,0:T(8,128)(2,1)} copy(f16[3,8,256,128]{2,3,1,0:T(8,128)(2,1)} %fusion.15) | data formatting | bytes 3145728 | tf_op jit(solution)/shard_map/convert_element_type | solution.py:32
  158.6 4.8 %gather_fusion.2 = f16[192,64,128]{2,1,0:T(8,128)(2,1)} fusion(f16[96,64,128]{2,1,0:T(8,128)(2,1)} %bitcast.109, s32[1024]{0:T(1024)S(1)} %pad_clamp_fusion), kind=kCustom, calls=%fused_computation.2 | custom fusion | bytes 6292224 | tf_op jit(solution)/shard_map/gather | solution.py:107
  163.4 4.2 %concatenate.6 = f16[32,400,128]{2,1,0:T(8,128)(2,1)} pad(f16[32,384,128]{2,1,0:T(8,128)(2,1)} %bitcast.111, f16[]{:T(256)S(6)} %convert_element_type.86), padding=0_0x0_16x0_0 | pad | bytes 6422530 | tf_op jit(solution)/shard_map/concatenate | solution.py:37
  167.6 4.8 %all-to-all-start.2 = ((f16[32,400,128]{2,1,0:T(8,128)(2,1)}), f16[32,400,128]{2,1,0:T(8,128)(2,1)}, u32[]{:S(2)}, u32[]{:S(2)}) async-start(f16[32,400,128]{2,1,0:T(8,128)(2,1)} %concatenate.6), calls=%async_computation.2 | async-start | bytes 6553600 | tf_op jit(solution)/shard_map/all_to_all | solution.py:110
  172.5 0.5 broadcast.369
  173.0 0.7 reduce.28
  173.7 0.1 eq.49
  173.8 0.9 copy.166
  174.7 72.0 %all-to-all-done.2 = f16[32,400,128]{2,1,0:T(8,128)(2,1)} async-done(((f16[32,400,128]{2,1,0:T(8,128)(2,1)}), f16[32,400,128]{2,1,0:T(8,128)(2,1)}, u32[]{:S(2)}, u32[]{:S(2)}) %all-to-all-start.2) | async-done | bytes 3276832 | tf_op jit(solution)/shard_map/all_to_all | solution.py:110
  246.7 0.9 slice.28
  247.6 0.1 copy.200
  247.7 5.3 %convert_multiply_fusion.3 = f32[32,384,128]{2,1,0:T(8,128)} fusion(f16[32,400,128]{2,1,0:T(8,128)(2,1)} %all-to-all-done.2, f32[32]{0:T(128)S(1)} %exponential_bitcast_fusion), kind=kLoop, calls=%fused_computation.9 | loop fusion | flops 3145728 | bytes 9437312 | tf_op jit(solution)/shard_map/mul | solution.py:42
  253.0 7.2 %reshape.354 = f32[192,8192]{1,0:T(8,128)} reshape(f32[32,384,128]{2,1,0:T(8,128)} %convert_multiply_fusion.3) | data formatting | bytes 12582912 | tf_op jit(solution)/shard_map/reshape | solution.py:117
  260.2 5.9 %abs_reduce_fusion.1 = (f32[]{:T(128)}, f32[32,8192]{1,0:T(8,128)S(1)}) fusion(f32[192,8192]{1,0:T(8,128)} %reshape.354, s32[192]{0:T(256)S(1)} %eq.49), kind=kOutput, calls=%fused_computation.33 | convolution fusion | flops 604510208 | bytes 7340804 | tf_op jit(solution)/shard_map/dot_general | solution.py:115
  266.8 0.9 multiply_convert_fusion.1
  267.7 1.3 convert_element_type.90
  269.0 0.1 concatenate.7
  269.2 15.4 %all-gather.1 = f16[4,2064,128]{2,1,0:T(8,128)(2,1)S(1)} all-gather(f16[1,2064,128]{2,1,0:T(8,128)(2,1)S(1)} %concatenate.7), channel_id=1, replica_groups=mesh['shard'=8,'rep'=4] {'rep'}, dimensions={0}, use_global_device_ids=true | all-gather | bytes 2641920 | tf_op jit(solution)/shard_map/all_gather | solution.py:122
  284.6 0.1 fusion.54
  284.7 0.5 multiply_multiply_fusion
  285.2 2.3 copy.169
  (26 shorter events, 0.2 us)
Async XLA Ops:
  7.2 9.4 %copy-start = (bf16[8192,128]{1,0:T(8,128)(2,1)S(1)}, bf16[8192,128]{1,0:T(8,128)(2,1)}, u32[]{:S(2)}) copy-start(bf16[8192,128]{1,0:T(8,128)(2,1)} %param.5) | copy-start | bytes 6291460
  9.2 14.4 %all-to-all-start = ((s32[32,1,6]{2,1,0:T(1,128)}), s32[32,1,6]{2,1,0:T(1,128)S(1)}, u32[]{:S(2)}, u32[]{:S(2)}) async-start(s32[32,1,6]{2,1,0:T(1,128)} %bitcast.1), calls=%async_computation | async-start | bytes 32768 | tf_op jit(solution)/shard_map/all_to_all | solution.py:68
  17.3 9.6 %copy-start.3 = (f32[128,128]{1,0:T(8,128)}, f32[128,128]{1,0:T(8,128)S(1)}, u32[]{:S(2)}) copy-start(f32[128,128]{1,0:T(8,128)S(1)} %fusion.56) | copy-start | bytes 196612
  26.9 5.3 %copy-start.4 = (s32[3,8]{1,0:T(4,128)S(1)}, s32[3,8]{1,0:T(4,128)}, u32[]{:S(2)}) copy-start(s32[3,8]{1,0:T(4,128)} %param.3) | copy-start | bytes 292
  26.9 77.1 %all-to-all-start.1 = ((bf16[8,6,256,128]{3,2,1,0:T(8,128)(2,1)}), bf16[8,6,256,128]{3,2,1,0:T(8,128)(2,1)}, u32[]{:S(2)}, u32[]{:S(2)}) async-start(bf16[8,6,256,128]{3,2,1,0:T(8,128)(2,1)} %bitcast.110), calls=%async_computation.1 | async-start | bytes 6291456 | tf_op jit(solution)/shard_map/all_to_all | solution.py:82
  31.5 98.1 %all-reduce.4.cloned.1.call-start = ((), (), s32[]{:S(2)}) async-start(), calls=%async_computation.3 | async-start | bytes 131072 | tf_op jit(solution)/shard_map/psum | solution.py:81
  131.2 5.1 %copy-start.2 = (f32[128,128]{1,0:T(8,128)S(1)}, f32[128,128]{1,0:T(8,128)}, u32[]{:S(2)}) copy-start(f32[128,128]{1,0:T(8,128)} %all-reduce.4.cloned.1.call-done) | copy-start | bytes 196612
  138.8 5.2 %copy-start.1 = (f32[3,256,128]{1,2,0:T(8,128)S(1)}, f32[3,256,128]{1,2,0:T(8,128)}, u32[]{:S(2)}) copy-start(f32[3,256,128]{1,2,0:T(8,128)} %multiply_add_fusion.1) | copy-start | bytes 1179652
  167.6 79.1 %all-to-all-start.2 = ((f16[32,400,128]{2,1,0:T(8,128)(2,1)}), f16[32,400,128]{2,1,0:T(8,128)(2,1)}, u32[]{:S(2)}, u32[]{:S(2)}) async-start(f16[32,400,128]{2,1,0:T(8,128)(2,1)} %concatenate.6), calls=%async_computation.2 | async-start | bytes 6553600 | tf_op jit(solution)/shard_map/all_to_all | solution.py:110
Sparse Core Ops, SparseCore 0:
  36.3 93.2 all-reduce.3

commit v3 on v2

--- a/solution.py
+++ b/solution.py
@@ -76,7 +76,7 @@
     incoming = lax.dynamic_index_in_dim(
         named.reshape(shards, reps, slots), lax.axis_index("rep"), axis=1, keepdims=False
     )
-    after_gram = (local_gram[0, 0] < 0).astype(jnp.int32)
+    after_gram = (jnp.min(jnp.max(local_gram, axis=1)) < 0).astype(jnp.int32)
     wanted = table[jnp.maximum(incoming, 0) + after_gram]
     gram = lax.psum(local_gram, "shard")
     replies = lax.all_to_all(wanted, "shard", split_axis=0, concat_axis=0, tiled=True)

time: 295 us -> 295 us (level)
  no operation moved by 1% of the time
where the time goes in v3:
time: 295 us; the launch traced here: 294 us
  waiting for transfers between devices  157 us (53%)
  local copies, waits for them, and re-layouts  38.9 us (13%)
  matrix products  34.6 us (12%)
  starting transfers between devices  16.8 us (6%)
  between operations  16.4 us (6%)
  blocking collectives  15.4 us (5%)
  other arithmetic  15 us (5%)
    all_to_all x1, waiting for transfers between devices, per_device(): lax.all_to_all(outgoing, ('shard', 'rep'), split_axis=0, concat_axis=0, t...  72 us
    all_to_all x1, waiting for transfers between devices, per_device(): lax.all_to_all(wanted, 'shard', split_axis=0, concat_axis=0, tiled=True)  66.1 us
    all_gather x1, blocking collectives, per_device(): lax.all_gather(with_level(coded[None], level)[0], 'rep', axis=0, tiled=Fa...  15.4 us
    dot_general x3, matrix products, apply_system(): jnp.einsum('bktl,bklr->btr', weighted, fetched, preferred_element_type=jn...  14.5 us
    psum x1, waiting for transfers between devices, per_device(): gram = lax.psum(local_gram, 'shard')  13.9 us
    all_to_all x1, starting transfers between devices, per_device(): lax.all_to_all(requests.reshape(shards * reps, slots), ('shard', 'rep'),...  7.33 us
    reshape x1, local copies, waits for them, and re-layouts, per_device(): back.reshape(shards * reps * slots, part * rank)  7.15 us
    dot_general x1, matrix products, per_device(): jnp.dot(selector, back.reshape(shards * reps * slots, part * rank), preci...  5.95 us
  transfers between devices with their start and end apart: 4, of which 4 were waited for; matrix products, arithmetic and copies ran while one was open for 7% of the time, Pallas kernels for 0%

profile of v3, /device:TPU:0, one launch (start us, length us, event | category | flops | bytes accessed | tf_op | source)
XLA Modules:
  0.0 294.3 jit_solution(13309468336662940046)
XLA Ops:
  7.2 0.0 copy-start
  7.2 0.9 reshape.342
  8.1 0.1 fusion.50
  8.2 0.2 select_reduce_fusion.1
  8.4 0.1 select_reduce_fusion
  8.5 0.1 sub.47
  8.6 0.6 broadcast_in_dim.16
  9.2 7.3 %all-to-all-start = ((s32[32,1,6]{2,1,0:T(1,128)}), s32[32,1,6]{2,1,0:T(1,128)S(1)}, u32[]{:S(2)}, u32[]{:S(2)}) async-start(s32[32,1,6]{2,1,0:T(1,128)} %bitcast.1), calls=%async_computation | async-start | bytes 32768 | tf_op jit(solution)/shard_map/all_to_all | solution.py:68
  16.6 0.0 copy-done
  16.6 1.4 fusion.56
  18.0 0.7 reduce_min.9
  19.3 4.3 %all-to-all-done = s32[32,1,6]{2,1,0:T(1,128)S(1)} async-done(((s32[32,1,6]{2,1,0:T(1,128)}), s32[32,1,6]{2,1,0:T(1,128)S(1)}, u32[]{:S(2)}, u32[]{:S(2)}) %all-to-all-start) | async-done | bytes 800 | tf_op jit(solution)/shard_map/all_to_all | solution.py:68
  23.7 0.1 copy.209
  23.8 0.2 add_reduce_fusion
  24.0 0.1 copy.155
  24.1 0.1 reshape.355
  24.2 2.7 gather_fusion
  26.9 4.6 %all-to-all-start.1 = ((bf16[8,6,256,128]{3,2,1,0:T(8,128)(2,1)}), bf16[8,6,256,128]{3,2,1,0:T(8,128)(2,1)}, u32[]{:S(2)}, u32[]{:S(2)}) async-start(bf16[8,6,256,128]{3,2,1,0:T(8,128)(2,1)} %bitcast.110), calls=%async_computation.1 | async-start | bytes 6291456 | tf_op jit(solution)/shard_map/all_to_all | solution.py:82
  31.5 0.0 all-reduce.4.cloned.1.call-start
  31.5 0.7 all-reduce.4.cloned.1.call-update
  32.2 0.1 reshape.345
  32.3 0.6 iota_reduce_fusion
  32.9 0.1 mul.201
  33.0 0.1 add.247
  33.1 4.7 %copy.160 = bf16[3,8,256,256]{2,3,1,0:T(8,128)(2,1)} copy(bf16[3,8,256,256]{3,2,1,0:T(8,128)(2,1)} %param.4) | data formatting | bytes 6291456 | tf_op args[1]
  37.8 66.1 %all-to-all-done.1 = bf16[8,6,256,128]{3,2,1,0:T(8,128)(2,1)} async-done(((bf16[8,6,256,128]{3,2,1,0:T(8,128)(2,1)}), bf16[8,6,256,128]{3,2,1,0:T(8,128)(2,1)}, u32[]{:S(2)}, u32[]{:S(2)}) %all-to-all-start.1) | async-done | bytes 3145760 | tf_op jit(solution)/shard_map/all_to_all | solution.py:82
  104.0 3.8 %gather_fusion.1 = bf16[24,256,128]{2,1,0:T(8,128)(2,1)} fusion(bf16[48,256,128]{2,1,0:T(8,128)(2,1)} %bitcast.4, s32[1024]{0:T(1024)S(1)} %pad_clamp_fusion.1), kind=kCustom, calls=%fused_computation.1 | custom fusion | bytes 3145824 | tf_op jit(solution)/shard_map/gather | solution.py:83
  107.8 3.5 %convolution_bitcast_fusion = f32[3,256,128]{1,2,0:T(8,128)S(1)} fusion(bf16[3,8,256,128]{3,2,1,0:T(8,128)(2,1)} %bitcast.112, bf16[3,8,256,256]{3,2,1,0:T(8,128)(2,1)} %param.4), kind=kOutput, calls=%fused_computation.26 | convolution fusion | flops 402653184 | bytes 5111808 | tf_op jit(solution)/shard_map/bktl,bklr->btr/dot_general | solution.py:86
  111.4 4.3 %fusion.16 = f32[3,256,128]{1,2,0:T(8,128)S(1)} fusion(bf16[3,8,256,128]{3,2,1,0:T(8,128)(2,1)} %bitcast.113, bf16[3,8,256,256]{2,3,1,0:T(8,128)(2,1)} %copy.160, f32[3,256,128]{1,2,0:T(8,128)S(1)} %convolution_bitcast_fusion), kind=kOutput, calls=%fused_computation.20 | convolution fusion | flops 810123264 | bytes 5505024 | tf_op jit(solution)/shard_map/bktl,bklr->btr/dot_general | solution.py:16
  115.7 13.9 %all-reduce.4.cloned.1.call-done = f32[128,128]{0,1:T(8,128)} async-done(((f32[128,128]{0,1:T(8,128)}), f32[128,128]{0,1:T(8,128)}) %all-reduce.4.cloned.1.call-update) | async-done | bytes 65552 | tf_op jit(solution)/shard_map/psum | solution.py:81
  129.6 1.4 multiply_reduce_fusion.3
  131.0 0.1 multiply_reduce_fusion.2
  131.1 0.1 multiply_add_fusion.2
  131.2 5.1 %fusion.19 = f32[3,256,128]{1,2,0:T(8,128)} fusion(bf16[3,8,256,128]{3,2,1,0:T(8,128)(2,1)} %bitcast.114, bf16[3,8,256,256]{2,3,1,0:T(8,128)(2,1)} %copy.160, f32[3,256,128]{1,2,0:T(8,128)S(1)} %multiply_add_fusion.2), kind=kOutput, calls=%fused_computation.21 | convolution fusion | flops 810123264 | bytes 5505024 | tf_op jit(solution)/shard_map/bktl,bklr->btr/dot_general | solution.py:16
  136.2 1.5 multiply_reduce_fusion.1
  137.8 0.1 multiply_reduce_fusion
  137.9 0.8 multiply_add_fusion.1
  138.7 5.2 %fusion.22 = f32[3,256,128]{1,2,0:T(8,128)} fusion(bf16[3,8,256,128]{3,2,1,0:T(8,128)(2,1)} %bitcast.115, bf16[3,8,256,256]{2,3,1,0:T(8,128)(2,1)} %copy.160, f32[3,256,128]{1,2,0:T(8,128)} %multiply_add_fusion.1), kind=kOutput, calls=%fused_computation.22 | convolution fusion | flops 810123264 | bytes 5505024 | tf_op jit(solution)/shard_map/bktl,bklr->btr/dot_general | solution.py:16
  143.9 0.0 copy-done.1
  143.9 1.5 fusion.29
  145.5 1.1 multiply_add_fusion
  146.5 4.7 %abs_reduce_fusion = (f32[]{:T(128)}, f32[3,128,8,256]{3,1,2,0:T(8,128)}) fusion(bf16[3,8,256,256]{3,2,1,0:T(8,128)(2,1)} %param.4, f32[3,256,128]{1,2,0:T(8,128)S(1)} %multiply_add_fusion), kind=kOutput, calls=%fused_computation.15 | convolution fusion | flops 404324352 | bytes 6684676 | tf_op jit(solution)/shard_map/bktl,btr->bklr/dot_general | solution.py:100
  152.0 3.5 %fusion.15 = f16[3,8,256,128]{2,3,1,0:T(8,128)(2,1)} fusion(f32[3,128,8,256]{3,1,2,0:T(8,128)} %get-tuple-element.16, f32[]{:T(128)S(6)} %exp2.28), kind=kLoop, calls=%fused_computation.19 | loop fusion | flops 1572864 | bytes 4718596 | tf_op jit(solution)/shard_map/convert_element_type | solution.py:32
  155.5 3.0 %copy.175 = f16[3,8,256,128]{3,2,1,0:T(8,128)(2,1)} copy(f16[3,8,256,128]{2,3,1,0:T(8,128)(2,1)} %fusion.15) | data formatting | bytes 3145728 | tf_op jit(solution)/shard_map/convert_element_type | solution.py:32
  158.5 4.8 %gather_fusion.2 = f16[192,64,128]{2,1,0:T(8,128)(2,1)} fusion(f16[96,64,128]{2,1,0:T(8,128)(2,1)} %bitcast.109, s32[1024]{0:T(1024)S(1)} %pad_clamp_fusion), kind=kCustom, calls=%fused_computation.2 | custom fusion | bytes 6292224 | tf_op jit(solution)/shard_map/gather | solution.py:107
  163.3 4.2 %concatenate.6 = f16[32,400,128]{2,1,0:T(8,128)(2,1)} pad(f16[32,384,128]{2,1,0:T(8,128)(2,1)} %bitcast.111, f16[]{:T(256)S(6)} %convert_element_type.82), padding=0_0x0_16x0_0 | pad | bytes 6422530 | tf_op jit(solution)/shard_map/concatenate | solution.py:37
  167.5 4.8 %all-to-all-start.2 = ((f16[32,400,128]{2,1,0:T(8,128)(2,1)}), f16[32,400,128]{2,1,0:T(8,128)(2,1)}, u32[]{:S(2)}, u32[]{:S(2)}) async-start(f16[32,400,128]{2,1,0:T(8,128)(2,1)} %concatenate.6), calls=%async_computation.2 | async-start | bytes 6553600 | tf_op jit(solution)/shard_map/all_to_all | solution.py:110
  172.4 0.5 broadcast.369
  172.9 0.7 reduce.28
  173.6 0.1 eq.49
  173.7 0.9 copy.174
  174.6 72.0 %all-to-all-done.2 = f16[32,400,128]{2,1,0:T(8,128)(2,1)} async-done(((f16[32,400,128]{2,1,0:T(8,128)(2,1)}), f16[32,400,128]{2,1,0:T(8,128)(2,1)}, u32[]{:S(2)}, u32[]{:S(2)}) %all-to-all-start.2) | async-done | bytes 3276832 | tf_op jit(solution)/shard_map/all_to_all | solution.py:110
  246.6 0.9 slice.23
  247.5 0.1 copy.210
  247.6 5.3 %convert_multiply_fusion.3 = f32[32,384,128]{2,1,0:T(8,128)} fusion(f16[32,400,128]{2,1,0:T(8,128)(2,1)} %all-to-all-done.2, f32[32]{0:T(128)S(1)} %exponential_bitcast_fusion), kind=kLoop, calls=%fused_computation.9 | loop fusion | flops 3145728 | bytes 9437312 | tf_op jit(solution)/shard_map/mul | solution.py:42
  252.9 7.2 %reshape.350 = f32[192,8192]{1,0:T(8,128)} reshape(f32[32,384,128]{2,1,0:T(8,128)} %convert_multiply_fusion.3) | data formatting | bytes 12582912 | tf_op jit(solution)/shard_map/reshape | solution.py:117
  260.1 5.9 %abs_reduce_fusion.1 = (f32[]{:T(128)}, f32[32,8192]{1,0:T(8,128)S(1)}) fusion(f32[192,8192]{1,0:T(8,128)} %reshape.350, s32[192]{0:T(256)S(1)} %eq.49), kind=kOutput, calls=%fused_computation.33 | convolution fusion | flops 604510208 | bytes 7340804 | tf_op jit(solution)/shard_map/dot_general | solution.py:115
  266.8 0.9 multiply_convert_fusion.1
  267.6 1.3 convert_element_type.86
  269.0 0.1 concatenate.7
  269.1 15.4 %all-gather.1 = f16[4,2064,128]{2,1,0:T(8,128)(2,1)S(1)} all-gather(f16[1,2064,128]{2,1,0:T(8,128)(2,1)S(1)} %concatenate.7), channel_id=1, replica_groups=mesh['shard'=8,'rep'=4] {'rep'}, dimensions={0}, use_global_device_ids=true | all-gather | bytes 2641920 | tf_op jit(solution)/shard_map/all_gather | solution.py:122
  284.5 0.1 fusion.54
  284.6 0.5 multiply_multiply_fusion
  285.1 2.3 copy.177
  (24 shorter events, 0.2 us)
Async XLA Ops:
  7.2 9.4 %copy-start = (bf16[8192,128]{1,0:T(8,128)(2,1)S(1)}, bf16[8192,128]{1,0:T(8,128)(2,1)}, u32[]{:S(2)}) copy-start(bf16[8192,128]{1,0:T(8,128)(2,1)} %param.5) | copy-start | bytes 6291460
  9.2 14.4 %all-to-all-start = ((s32[32,1,6]{2,1,0:T(1,128)}), s32[32,1,6]{2,1,0:T(1,128)S(1)}, u32[]{:S(2)}, u32[]{:S(2)}) async-start(s32[32,1,6]{2,1,0:T(1,128)} %bitcast.1), calls=%async_computation | async-start | bytes 32768 | tf_op jit(solution)/shard_map/all_to_all | solution.py:68
  26.9 5.3 %copy-start.3 = (s32[3,8]{1,0:T(4,128)S(1)}, s32[3,8]{1,0:T(4,128)}, u32[]{:S(2)}) copy-start(s32[3,8]{1,0:T(4,128)} %param.3) | copy-start | bytes 292
  26.9 77.1 %all-to-all-start.1 = ((bf16[8,6,256,128]{3,2,1,0:T(8,128)(2,1)}), bf16[8,6,256,128]{3,2,1,0:T(8,128)(2,1)}, u32[]{:S(2)}, u32[]{:S(2)}) async-start(bf16[8,6,256,128]{3,2,1,0:T(8,128)(2,1)} %bitcast.110), calls=%async_computation.1 | async-start | bytes 6291456 | tf_op jit(solution)/shard_map/all_to_all | solution.py:82
  31.5 98.1 %all-reduce.4.cloned.1.call-start = ((), (), s32[]{:S(2)}) async-start(), calls=%async_computation.3 | async-start | bytes 131072 | tf_op jit(solution)/shard_map/psum | solution.py:81
  131.2 5.1 %copy-start.2 = (f32[128,128]{0,1:T(8,128)S(1)}, f32[128,128]{0,1:T(8,128)}, u32[]{:S(2)}) copy-start(f32[128,128]{0,1:T(8,128)} %all-reduce.4.cloned.1.call-done) | copy-start | bytes 196612
  138.7 5.2 %copy-start.1 = (f32[3,256,128]{1,2,0:T(8,128)S(1)}, f32[3,256,128]{1,2,0:T(8,128)}, u32[]{:S(2)}) copy-start(f32[3,256,128]{1,2,0:T(8,128)} %multiply_add_fusion.1) | copy-start | bytes 1179652
  167.5 79.1 %all-to-all-start.2 = ((f16[32,400,128]{2,1,0:T(8,128)(2,1)}), f16[32,400,128]{2,1,0:T(8,128)(2,1)}, u32[]{:S(2)}, u32[]{:S(2)}) async-start(f16[32,400,128]{2,1,0:T(8,128)(2,1)} %concatenate.6), calls=%async_computation.2 | async-start | bytes 6553600 | tf_op jit(solution)/shard_map/all_to_all | solution.py:110
Sparse Core Ops, SparseCore 0:
  36.3 93.2 all-reduce.3
